TPU v7x, 32 devices: a whole 2x2x4 slice. The times are simulated.
32 devices in a mesh: ctx: 8 (over z, y), req: 4 (over x, core).
Axes of the slice: x: 2, y: 2, z: 4, core: 2. Of those that a mesh axis runs over, the one named last changes fastest.
Arguments:
- queries: bfloat16 [4096, 1024], P(('req', 'ctx')), parts along dimension 0, may hold values from -6 to 6
- keys: bfloat16 [4096, 256], P(('req', 'ctx')), parts along dimension 0, may hold values from -6 to 6
- lse: float32 [16, 4096], P(None, ('req', 'ctx')), parts along dimension 1, may hold values from -0.5 to 15, as said below
- length: int32 [4], P('req'), parts along dimension 0, may hold values from 512 to 1024
Outputs:
- key_scores: float32 [16, 4096], P(None, ('req', 'ctx')), parts along dimension 1
There are 4 independent parts, one for each index of `req`. A program takes and returns all parts, laid end to end along the dimension named above; each array names one. Nothing has to cross between parts.
Inputs may be any that keep to these rules, and one draw needn't show every extreme that they name: lse[h, i] is the logarithm of i + 1 plus an offset between -0.5 and 3.
All inputs are finite; a program needn't handle non-finite values.
Results may differ from a plain program's by a relative error of at most 0.0003.
Values may be sent and summed in bfloat16 or wider, within the bound.
No kernel may reach another device: no remote copies, remote signals or barrier semaphores. Data moves between devices by JAX's collectives and lax.ppermute only.
A program may use at most 64 MiB of HBM per device.

v0:
```python
import math

import jax
import jax.numpy as jnp
from jax import lax
from jax.sharding import PartitionSpec as P

HEAD_DIM = 64


def block_terms(query_set, lse_set, positions, key_block, key_start, limit):
    heads = lse_set.shape[0]
    rows_here = query_set.shape[0]
    width = key_block.shape[0]
    kv_heads = key_block.shape[1] // HEAD_DIM
    grouped = query_set.reshape(rows_here, kv_heads, heads // kv_heads, HEAD_DIM)
    key_view = key_block.reshape(width, kv_heads, HEAD_DIM)
    logits = jnp.einsum("rhgd,chd->hgrc", grouped, key_view, preferred_element_type=jnp.float32)
    logits = logits.reshape(heads, rows_here, width) * HEAD_DIM ** (-0.5)
    key_pos = key_start + jnp.arange(width, dtype=jnp.int32)
    valid = (positions[:, None] >= key_pos[None, :]) & (positions[:, None] < limit)
    weights = jnp.where(valid[None], jnp.exp(logits - lse_set[:, :, None]), jnp.float32(0.0))
    return jnp.sum(weights, axis=1)


def make_absorb(query_sets, limit, heads, total, piece, start):
    width = piece.shape[0]
    step_len = math.gcd(width, 512)
    turns = width // step_len

    def skipped(*operands):
        return jnp.zeros((heads, step_len), jnp.float32)

    def one_turn(turn, running):
        offset = turn * step_len
        key_block = lax.dynamic_slice_in_dim(piece, offset, step_len, 0)
        key_start = start + offset
        part_sum = jnp.zeros((heads, step_len), jnp.float32)
        for query_set, lse_set, positions in query_sets:
            needed = (key_start <= jnp.max(positions)) & (key_start < limit)
            part_sum = lax.cond(
                needed,
                block_terms,
                skipped,
                query_set,
                lse_set,
                positions,
                key_block,
                key_start,
                limit,
            )
        current = lax.dynamic_slice(running, (0, key_start), (heads, step_len))
        return lax.dynamic_update_slice(running, current + part_sum, (0, key_start))

    return lax.fori_loop(0, turns, one_turn, total)


def shards(queries, keys, lse, length):
    tok_rows = queries.shape[0]
    heads = lse.shape[0]
    devices_ctx = lax.axis_size("ctx")
    my_index = lax.axis_index("ctx")
    limit = length[0]
    first_row = my_index * tok_rows
    query_sets = [(queries, lse, first_row + jnp.arange(tok_rows, dtype=jnp.int32))]
    empty = jnp.zeros((heads, tok_rows * devices_ctx), jnp.float32)
    totals = make_absorb(
        query_sets,
        limit,
        heads,
        empty,
        lax.all_gather(keys, "ctx", axis=0, tiled=True),
        jnp.int32(0),
    )
    return lax.psum_scatter(totals, "ctx", scatter_dimension=1, tiled=True)


def solution(mesh):
    placed = (P(("req", "ctx"), None), P(("req", "ctx"), None), P(None, ("req", "ctx")), P("req"))
    return jax.shard_map(
        shards, mesh=mesh, in_specs=placed, out_specs=P(None, ("req", "ctx")), check_vma=False
    )
```

profile of v0, /device:TPU:0, one launch (start us, length us, event | category | flops | bytes accessed | tf_op | source)
XLA Modules:
  0.0 107.6 jit_solution(11371074071570174559)
XLA Ops:
  6.5 0.0 reduce-scatter.2.cloned.1.call-start
  6.5 0.7 add_reduce_fusion
  7.2 0.9 copy.5
  8.2 0.0 copy-start.1
  8.2 1.1 %copy.6 = bf16[128,1024]{0,1:T(8,128)(2,1)S(1)} copy(bf16[128,1024]{1,0:T(8,128)(2,1)} %param.8) | data formatting | bytes 524288
  9.3 29.6 %all_gather.3 = bf16[1024,256]{0,1:T(8,128)(2,1)S(1)} all-gather(bf16[128,256]{0,1:T(8,128)(2,1)S(1)} %copy.5), channel_id=1, replica_groups=mesh['ctx'=8,'req'=4] {'ctx'}, dimensions={0}, use_global_device_ids=true | all-gather | bytes 589824 | tf_op jit(solution)/shard_map/all_gather | solution.py:72
  38.9 0.0 copy-done.1
  38.9 4.9 %while.15 = (s32[]{:T(128)}, f32[16,1024]{1,0:T(8,128)S(1)}, s32[]{:T(128)}, s32[]{:T(128)}, bf16[1024,256]{0,1:T(8,128)(2,1)S(1)}, /*index=5*/bf16[128,1024]{0,...) while((s32[]{:T(128)}, f32[16,1024]{1,0:T(8,128)S(1)}, ...), condition=%wide.region_5.6_spmd.clone, body=%wide.region_1.5_spmd.clone.sunk | while | flops 138543888 | bytes 1391129 | solution.py:55
  40.2 2.2 %conditional.3 = (f32[16,512]{1,0:T(8,128)S(1)}) conditional(s32[]{:T(128)} %convert_element_type.10, () %tuple.49, (s32[]{:T(128)}, s32[]{:T(128)}, s32[]{:T(128)}, bf16[1024,256]{0,1:T(8,128)(2,1)S(1)}, s32[]{:T(128)}, /*index=5*/bf16[128,1024]{0,1:T(8,128)(2,1)S(1)}, f32[16,128]{1,0:T(8,128)S(1)}, s32[128]{0:T(128)S(1)}) %tuple.50), branch_computations={%region_2.0_spmd, %region_3.4_spmd} | conditional | flops 138535680 | bytes 1292056 | solution.py:41
  40.2 0.7 broadcast_compare_fusion
  40.9 0.1 compare_and_fusion
  41.0 1.4 %fusion.4 = f32[4,4,512]{2,1,0:T(4,128)S(1)} fusion(bf16[512,4,64,1]{0,2,3,1:T(8,128)(2,1)S(1)} %bitcast.18, bf16[128,4,4,64]{0,3,2,1:T(8,128)(2,1)S(1)} %bitcast.19, f32[4,4,128]{2,1,0:T(4,128)S(1)} %bitcast.20, pred[128,512]{1,0:T(8,128)(4,1)S(1)} %compare_and_fusion), kind=kOutput, calls=%fused_computation.4 | convolution fusion | flops 138403840 | bytes 630784 | tf_op jit(solution)/shard_map/while/body/eval_jaxpr/cond/branch_1_fun/rhgd,chd->hgrc/dot_general | solution.py:18
  43.8 0.0 copy-start
  43.8 0.6 copy-done
  44.4 0.0 reduce-scatter.2.cloned.1.call-update
  44.5 56.3 %reduce-scatter.2.cloned.1.call-done = f32[16,128]{1,0:T(8,128)} async-done(((f32[16,1024]{1,0:T(8,128)}), f32[16,128]{1,0:T(8,128)}) %reduce-scatter.2.cloned.1.call-update) | async-done | bytes 8208 | tf_op jit(solution)/shard_map/reduce_scatter | solution.py:75
  (10 shorter events, 0.1 us)
Async XLA Ops:
  6.5 94.3 %reduce-scatter.2.cloned.1.call-start = ((), (), s32[]{:S(2)}) async-start(), calls=%async_computation.1 | async-start | bytes 73728 | tf_op jit(solution)/shard_map/reduce_scatter | solution.py:75
  8.2 30.7 %copy-start.1 = (f32[16,128]{1,0:T(8,128)S(1)}, f32[16,128]{1,0:T(8,128)}, u32[]{:S(2)}) copy-start(f32[16,128]{1,0:T(8,128)} %param.10) | copy-start | bytes 24580
  43.8 0.6 copy-start
Sparse Core Ops, SparseCore 0:
  44.6 56.1 reduce-scatter.1
where the time goes:
time: 108 us
  waiting for transfers between devices  56.3 us (52%)
  blocking collectives  29.6 us (27%)
  between operations  13.4 us (12%)
  local copies, waits for them, and re-layouts  2.75 us (3%)
  loops' own time  2.73 us (3%)
  other arithmetic  1.46 us (1%)
  matrix products  1.35 us (1%)
    reduce_scatter x1, waiting for transfers between devices, shards(): return lax.psum_scatter(totals, 'ctx', scatter_dimension=1, tiled=True)  56.3 us
    all_gather x1, blocking collectives, shards(): lax.all_gather(keys, 'ctx', axis=0, tiled=True)  29.6 us
    unnamed x6, local copies, waits for them, and re-layouts  2.69 us
    another operation x1, loops' own time, make_absorb(): return lax.fori_loop(0, turns, one_turn, total)  2.66 us
  transfers between devices with their start and end apart: 1, of which 1 were waited for; matrix products, arithmetic and copies ran while one was open for 0% of the time, Pallas kernels for 0%

commit v1 on v0

v1 whole, which is shorter than its diff:
```python
import functools

import jax
import jax.numpy as jnp
from jax import lax
from jax.experimental import pallas as pl
from jax.experimental.pallas import tpu as pltpu
from jax.sharding import PartitionSpec as P


HEAD_DIM = 64
LANES = 128
LOG2E = 1.4426950408889634
MASKED = 1e30
VMEM_BYTES = 12 * 1024 * 1024


def spread_offsets(lse_ref, offset_ref, block_index, limit):
    heads, rows = lse_ref.shape
    row = block_index * rows + lax.broadcasted_iota(jnp.int32, (heads, rows), 1)
    columns = jnp.where(row < limit, lse_ref[...] * LOG2E, MASKED).T
    for head in range(heads):
        offset_ref[head] = jnp.broadcast_to(columns[:, head : head + 1], offset_ref.shape[1:])


def add_block(key_ref, query_refs, offset_refs, out_ref, diagonal=False):
    width = key_ref.shape[0]
    heads = out_ref.shape[0]
    group = heads * HEAD_DIM // key_ref.shape[1]
    scale = HEAD_DIM ** (-0.5) * LOG2E
    low = lax.broadcasted_iota(jnp.int32, (width, LANES), 1) < HEAD_DIM
    if diagonal:
        rows = query_refs[0].shape[0]
        causal = lax.broadcasted_iota(jnp.int32, (rows, width), 0) >= lax.broadcasted_iota(jnp.int32, (rows, width), 1)
    for tile in range(key_ref.shape[1] // LANES):
        straight = key_ref[:, tile * LANES : (tile + 1) * LANES].astype(jnp.float32)
        swapped = pltpu.roll(straight, HEAD_DIM, 1)
        for half in range(LANES // HEAD_DIM):
            left, right = (straight, swapped) if half == 0 else (swapped, straight)
            spread = jnp.concatenate([jnp.where(low, left, 0.0), jnp.where(low, 0.0, right)], axis=0)
            spread = spread.astype(jnp.bfloat16)
            first_head = (2 * tile + half) * group
            for head in range(first_head, first_head + group, 2):
                lanes = slice(head * HEAD_DIM, (head + 2) * HEAD_DIM)
                sums = [0.0, 0.0]
                for query_ref, offset_ref in zip(query_refs, offset_refs):
                    logits = lax.dot_general(
                        query_ref[:, lanes], spread, (((1,), (1,)), ((), ())), preferred_element_type=jnp.float32
                    )
                    for side in range(2):
                        part = logits[:, side * width : (side + 1) * width]
                        weights = jnp.exp2(part * scale - offset_ref[head + side])
                        if diagonal:
                            weights = jnp.where(causal, weights, 0.0)
                        sums[side] += jnp.sum(weights, axis=0, keepdims=True)
                for side in range(2):
                    out_ref[head + side : head + side + 1, :] += sums[side]


def local_kernel(length_ref, lse_hbm, query_hbm, key_hbm, lse_1_ref, own_ref, offset_ref, offset_1_ref, query_ref, key_ref, lse_ref, sems):
    copies = [
        pltpu.make_async_copy(source, target, sems.at[at])
        for at, (source, target) in enumerate([(lse_hbm, lse_ref), (key_hbm, key_ref), (query_hbm, query_ref)])
    ]
    for copy in copies:
        copy.start()
    me = lax.axis_index("ctx")
    limit = length_ref[0]
    spread_offsets(lse_1_ref, offset_1_ref, me ^ 1, limit)
    copies[0].wait()
    spread_offsets(lse_ref, offset_ref, me, limit)
    own_ref[...] = jnp.zeros_like(own_ref)
    copies[1].wait()
    copies[2].wait()
    add_block(key_ref, [query_ref], [offset_ref], own_ref, diagonal=True)


def pair_kernel(xor, query_ref, query_1_ref, offset_ref, offset_1_ref, key_ref, out_ref):
    me = lax.axis_index("ctx")
    out_ref[...] = jnp.zeros_like(out_ref)

    @pl.when((me ^ xor) < me)
    def _():
        add_block(key_ref, [query_ref, query_1_ref], [offset_ref, offset_1_ref], out_ref)


def near_kernel(xor, query_ref, query_1_ref, offset_ref, offset_1_ref, key_x_ref, own_in_ref, key_ref, out_ref, own_ref):
    me = lax.axis_index("ctx")
    pair_kernel(xor, query_ref, query_1_ref, offset_ref, offset_1_ref, key_x_ref, out_ref)
    own_ref[...] = own_in_ref[...]

    @pl.when((me ^ 1) > me)
    def _():
        add_block(key_ref, [query_1_ref], [offset_1_ref], own_ref)


def call(body, out_shapes, operands, pairs, in_specs=None, scratch=()):
    heads, rows, width = out_shapes[0].shape[0], operands[-1].shape[0], LANES
    vmem = pl.BlockSpec(memory_space=pltpu.VMEM)
    return pl.pallas_call(
        body,
        out_shape=out_shapes,
        in_specs=in_specs or [vmem] * len(operands),
        out_specs=[vmem] * len(out_shapes),
        scratch_shapes=scratch,
        cost_estimate=pl.CostEstimate(
            flops=2 * pairs * heads * rows * width * HEAD_DIM,
            bytes_accessed=sum(x.size * x.dtype.itemsize for x in operands),
            transcendentals=pairs * heads * rows * width,
        ),
        compiler_params=pltpu.CompilerParams(vmem_limit_bytes=VMEM_BYTES),
    )(*operands)


def far_xors(devices_ctx):
    return list(range(devices_ctx - 2, 2, -2))


def shards(queries, keys, lse, length):
    devices_ctx = lax.axis_size("ctx")
    heads, rows = lse.shape
    sums = jax.ShapeDtypeStruct((heads, keys.shape[0]), jnp.float32)
    offsets = jax.ShapeDtypeStruct((heads, rows, LANES), jnp.float32)

    def swap(x, bit):
        return lax.ppermute(x, "ctx", [(i, i ^ bit) for i in range(devices_ctx)])

    xors = far_xors(devices_ctx)
    lse_1 = swap(lse, 1)
    queries_1 = swap(queries, 1)
    keys_x = {x: swap(keys, x) for x in xors + [2]}

    hbm, vmem, smem = (pl.BlockSpec(memory_space=space) for space in (pltpu.HBM, pltpu.VMEM, pltpu.SMEM))
    own, offset, offset_1, queries, keys = call(
        local_kernel,
        [sums, offsets, offsets, queries, keys],
        [length] + [pltpu.with_memory_space_constraint(x, pltpu.HBM) for x in (lse, queries, keys)] + [lse_1],
        1,
        [smem, hbm, hbm, hbm, vmem],
        [pltpu.VMEM(lse.shape, lse.dtype), pltpu.SemaphoreType.DMA((3,))],
    )
    both = [queries, queries_1, offset, offset_1]
    back = []
    for x in xors:
        (part,) = call(functools.partial(pair_kernel, x), [sums], both + [keys_x[x]], 2)
        back.append(swap(part, x))
    part, own = call(functools.partial(near_kernel, 2), [sums, sums], both + [keys_x[2], own, keys], 3)
    back.append(swap(part, 2))
    for term in back:
        own = own + term
    return own


def solution(mesh):
    placed = (P(("req", "ctx"), None), P(("req", "ctx"), None), P(None, ("req", "ctx")), P("req"))

    return jax.shard_map(shards, mesh=mesh, in_specs=placed, out_specs=P(None, ("req", "ctx")), check_vma=False)
```

time: 108 us -> 23.5 us (0.22)
  waiting for transfers between devices: 56.3 us -> 6.78 us
  blocking collectives: 29.6 us -> 0 us
  starting transfers between devices: 0.01 us -> 13.1 us
  between operations: 13.4 us -> 0.69 us
  local copies, waits for them, and re-layouts: 2.75 us -> 0 us
  loops' own time: 2.73 us -> 0 us
  Pallas kernels: 0 us -> 2.06 us
  matrix products: 1.35 us -> 0 us
    reduce_scatter x1 -> x0, waiting for transfers between devices: 56.3 us -> none  [shards(): return lax.psum_scatter(totals, 'ctx', scatter_dimension=1, tiled=True)]
    all_gather x1 -> x0, blocking collectives: 29.6 us -> none  [shards(): lax.all_gather(keys, 'ctx', axis=0, tiled=True)]
    ppermute x0 -> x8, starting transfers between devices: none -> 13.1 us  [swap(): return lax.ppermute(x, 'ctx', [(i, i ^ bit) for i in range(devices_ctx)])]
    ppermute x0 -> x8, waiting for transfers between devices: none -> 6.78 us  [swap(): return lax.ppermute(x, 'ctx', [(i, i ^ bit) for i in range(devices_ctx)])]
    another operation x3 -> x0, loops' own time: 2.73 us -> none  [the longest x1 2.66 us: make_absorb(): return lax.fori_loop(0, turns, one_turn, total)]
    unnamed x6 -> x0, local copies, waits for them, and re-layouts: 2.69 us -> none
    pallas_call x0 -> x4, Pallas kernels: none -> 2.06 us  [call(): pl.pallas_call(body, out_shape=out_shapes, in_specs=in_specs or [vmem] *...]
    dot_general x1 -> x0, matrix products: 1.35 us -> none  [block_terms(): jnp.einsum('rhgd,chd->hgrc', grouped, key_view, preferred_element_type=jn...]
  transfers between devices with their start and end apart: 1 -> 8, of which waited for: 1 -> 3; matrix products, arithmetic and copies ran while one was open for 0% -> 0% of each run, Pallas kernels for 0% -> 9%
where the time goes in v1:
time: 23.5 us; the launch traced here: 23.3 us
  starting transfers between devices  13.1 us (56%)
  waiting for transfers between devices  6.78 us (29%)
  Pallas kernels  2.06 us (9%)
  between operations  0.69 us (3%)
  other arithmetic  0.6 us (3%)
    ppermute x8, starting transfers between devices, swap(): return lax.ppermute(x, 'ctx', [(i, i ^ bit) for i in range(devices_ctx)])  13.1 us
    ppermute x8, waiting for transfers between devices, swap(): return lax.ppermute(x, 'ctx', [(i, i ^ bit) for i in range(devices_ctx)])  6.78 us
    pallas_call x4, Pallas kernels, call(): pl.pallas_call(body, out_shape=out_shapes, in_specs=in_specs or [vmem] *...  2.06 us
    add x1, other arithmetic, shards(): own = own + term  0.6 us
  transfers between devices with their start and end apart: 8, of which 3 were waited for; matrix products, arithmetic and copies ran while one was open for 0% of the time, Pallas kernels for 9%

profile of v1, /device:TPU:0, one launch (start us, length us, event | category | flops | bytes accessed | tf_op | source)
XLA Modules:
  0.0 23.3 jit_solution(15133183048364926680)
XLA Ops:
  0.0 3.0 %collective-permute-start.1 = (bf16[128,1024]{1,0:T(8,128)(2,1)}, bf16[128,1024]{1,0:T(8,128)(2,1)S(1)}, u32[]{:S(2)}, u32[]{:S(2)}) collective-permute-start(bf16[128,1024]{1,0:T(8,128)(2,1)} %query_hbm.1), channel_id=1, source_target_pairs={{0,4},{4,0},{8,12},{12,8},{16,20},{20,16},{24,28},{28,24},{1,5},{5... | collective-permute-start | bytes 786440 | tf_op jit(solution)/shard_map/ppermute | solution.py:126
  3.0 1.6 %collective-permute-start.2 = (bf16[128,256]{1,0:T(8,128)(2,1)}, bf16[128,256]{1,0:T(8,128)(2,1)S(1)}, u32[]{:S(2)}, u32[]{:S(2)}) collective-permute-start(bf16[128,256]{1,0:T(8,128)(2,1)} %key_hbm.1), channel_id=1, source_target_pairs={{0,8},{4,12},{8,0},{12,4},{16,24},{20,28},{24,16},{28,20},{1,9},{5... | collective-permute-start | bytes 196616 | tf_op jit(solution)/shard_map/ppermute | solution.py:126
  4.6 2.5 %collective-permute-start.3 = (bf16[128,256]{1,0:T(8,128)(2,1)}, bf16[128,256]{1,0:T(8,128)(2,1)S(1)}, u32[]{:S(2)}, u32[]{:S(2)}) collective-permute-start(bf16[128,256]{1,0:T(8,128)(2,1)} %key_hbm.1), channel_id=1, source_target_pairs={{0,24},{4,28},{8,16},{12,20},{16,8},{20,12},{24,0},{28,4},{1,25},{... | collective-permute-start | bytes 196616 | tf_op jit(solution)/shard_map/ppermute | solution.py:126
  7.0 0.1 collective-permute-start.5
  7.2 0.5 %collective-permute-start = (f32[16,128]{1,0:T(8,128)}, f32[16,128]{1,0:T(8,128)S(1)}, u32[]{:S(2)}, u32[]{:S(2)}) collective-permute-start(f32[16,128]{1,0:T(8,128)} %lse_hbm.1), channel_id=1, source_target_pairs={{0,4},{4,0},{8,12},{12,8},{16,20},{20,16},{24,28},{28,24},{1,5},{5... | collective-permute-start | bytes 24584 | tf_op jit(solution)/shard_map/ppermute | solution.py:126
  8.3 2.7 %collective-permute-done.lse_1_ref = f32[16,128]{1,0:T(8,128)S(1)} collective-permute-done((f32[16,128]{1,0:T(8,128)}, f32[16,128]{1,0:T(8,128)S(1)}, u32[]{:S(2)}, u32[]{:S(2)}) %collective-permute-start) | collective-permute-done | bytes 8224 | tf_op jit(solution)/shard_map/ppermute | solution.py:126
  11.0 1.6 %shard_map.46 = (f32[16,128]{1,0:T(8,128)S(1)}, f32[16,128,128]{2,1,0:T(8,128)S(1)}, f32[16,128,128]{2,1,0:T(8,128)S(1)}, bf16[128,1024]{1,0:T(8,128)(2,1)S(1)}, bf16[128,256]{1,0:T(8,128)(2,1)S(1)}) custom-call(s32[1]{0:T(128)S(6)} %copy.5.length_ref, f32[16,128]{1,0:T(8,128)} %lse_hbm.1, bf16[128,1024]{1,0:T(8,128)(2,1)} %query_hbm.1, ...), custom_call_target="tpu_custom_call" | custom-call | flops 4194304 | bytes 344068 | tf_op jit(solution)/shard_map/pallas_call | solution.py:100
  12.7 0.0 collective-permute-done.2.key_x_ref
  12.7 0.0 collective-permute-done.1.query_1_ref
  12.7 0.4 %shard_map.47 = (f32[16,128]{1,0:T(8,128)S(1)}, f32[16,128]{1,0:T(8,128)S(1)}) custom-call(bf16[128,1024]{1,0:T(8,128)(2,1)S(1)} %get-tuple-element.12.query_ref, bf16[128,1024]{1,0:T(8,128)(2,1)S(1)} %collective-permute-done.1.query_1_ref, f32[16,128,128]{2,1,0:T(8,128)S(1)} %get-tuple-element.13.offset_ref, ...), custom_call_target="tpu_custom_call" | custom-call | flops 100663296 | bytes 2760704 | tf_op jit(solution)/shard_map/pallas_call | solution.py:100
  13.1 2.4 %collective-permute-start.7 = (f32[16,128]{1,0:T(8,128)S(1)}, f32[16,128]{1,0:T(8,128)S(1)}, u32[]{:S(2)}, u32[]{:S(2)}) collective-permute-start(f32[16,128]{1,0:T(8,128)S(1)} %get-tuple-element.18), channel_id=1, source_target_pairs={{0,8},{4,12},{8,0},{12,4},{16,24},{20,28},{24,16},{28,20},{1,9},{5... | collective-permute-start | bytes 24584 | tf_op jit(solution)/shard_map/ppermute | solution.py:126
  15.6 0.0 collective-permute-done.3.key_ref
  15.6 2.6 %collective-permute-start.4 = (f32[16,128]{1,0:T(8,128)S(1)}, f32[16,128]{1,0:T(8,128)S(1)}, u32[]{:S(2)}, u32[]{:S(2)}) collective-permute-start(f32[16,128]{1,0:T(8,128)S(1)} %shard_map.48), channel_id=1, source_target_pairs={{0,24},{4,28},{8,16},{12,20},{16,8},{20,12},{24,0},{28,4},{1,25},{... | collective-permute-start | bytes 24584 | tf_op jit(solution)/shard_map/ppermute | solution.py:126
  18.1 0.0 collective-permute-done.5.key_ref
  18.1 0.5 %collective-permute-start.6 = (f32[16,128]{1,0:T(8,128)S(1)}, f32[16,128]{1,0:T(8,128)S(1)}, u32[]{:S(2)}, u32[]{:S(2)}) collective-permute-start(f32[16,128]{1,0:T(8,128)S(1)} %shard_map.49), channel_id=1, source_target_pairs={{0,16},{4,20},{8,24},{12,28},{16,0},{20,4},{24,8},{28,12},{1,17},{... | collective-permute-start | bytes 24584 | tf_op jit(solution)/shard_map/ppermute | solution.py:126
  18.6 0.0 collective-permute-done.7
  18.6 2.4 %collective-permute-done.4 = f32[16,128]{1,0:T(8,128)S(1)} collective-permute-done((f32[16,128]{1,0:T(8,128)S(1)}, f32[16,128]{1,0:T(8,128)S(1)}, u32[]{:S(2)}, u32[]{:S(2)}) %collective-permute-start.4) | collective-permute-done | bytes 8224 | tf_op jit(solution)/shard_map/ppermute | solution.py:126
  21.0 1.7 %collective-permute-done.6 = f32[16,128]{1,0:T(8,128)S(1)} collective-permute-done((f32[16,128]{1,0:T(8,128)S(1)}, f32[16,128]{1,0:T(8,128)S(1)}, u32[]{:S(2)}, u32[]{:S(2)}) %collective-permute-start.6) | collective-permute-done | bytes 8224 | tf_op jit(solution)/shard_map/ppermute | solution.py:126
  22.7 0.6 %add_add_fusion = f32[16,128]{1,0:T(8,128)} fusion(f32[16,128]{1,0:T(8,128)S(1)} %collective-permute-done.7, f32[16,128]{1,0:T(8,128)S(1)} %collective-permute-done.6, f32[16,128]{1,0:T(8,128)S(1)} %get-tuple-element.17, f32[16,128]{1,0:T(8,128)S(1)} %collective-permute-done.4), kind=kLoop, calls=%fused_computation | loop fusion | flops 6144 | bytes 40960 | tf_op jit(solution)/shard_map/add | solution.py:150
  (2 shorter events, 0.0 us)
Async XLA Ops:
  0.0 12.7 %collective-permute-start.1 = (bf16[128,1024]{1,0:T(8,128)(2,1)}, bf16[128,1024]{1,0:T(8,128)(2,1)S(1)}, u32[]{:S(2)}, u32[]{:S(2)}) collective-permute-start(bf16[128,1024]{1,0:T(8,128)(2,1)} %query_hbm.1), channel_id=1, source_target_pairs={{0,4},{4,0},{8,12},{12,8},{16,20},{20,16},{24,28},{28,24},{1,5},{5... | collective-permute-start | bytes 786440 | tf_op jit(solution)/shard_map/ppermute | solution.py:126
  3.0 9.7 %collective-permute-start.2 = (bf16[128,256]{1,0:T(8,128)(2,1)}, bf16[128,256]{1,0:T(8,128)(2,1)S(1)}, u32[]{:S(2)}, u32[]{:S(2)}) collective-permute-start(bf16[128,256]{1,0:T(8,128)(2,1)} %key_hbm.1), channel_id=1, source_target_pairs={{0,8},{4,12},{8,0},{12,4},{16,24},{20,28},{24,16},{28,20},{1,9},{5... | collective-permute-start | bytes 196616 | tf_op jit(solution)/shard_map/ppermute | solution.py:126
  4.6 11.0 %collective-permute-start.3 = (bf16[128,256]{1,0:T(8,128)(2,1)}, bf16[128,256]{1,0:T(8,128)(2,1)S(1)}, u32[]{:S(2)}, u32[]{:S(2)}) collective-permute-start(bf16[128,256]{1,0:T(8,128)(2,1)} %key_hbm.1), channel_id=1, source_target_pairs={{0,24},{4,28},{8,16},{12,20},{16,8},{20,12},{24,0},{28,4},{1,25},{... | collective-permute-start | bytes 196616 | tf_op jit(solution)/shard_map/ppermute | solution.py:126
  7.0 11.1 %collective-permute-start.5 = (bf16[128,256]{1,0:T(8,128)(2,1)}, bf16[128,256]{1,0:T(8,128)(2,1)S(1)}, u32[]{:S(2)}, u32[]{:S(2)}) collective-permute-start(bf16[128,256]{1,0:T(8,128)(2,1)} %key_hbm.1), channel_id=1, source_target_pairs={{0,16},{4,20},{8,24},{12,28},{16,0},{20,4},{24,8},{28,12},{1,17},{... | collective-permute-start | bytes 196616 | tf_op jit(solution)/shard_map/ppermute | solution.py:126
  7.2 3.9 %collective-permute-start = (f32[16,128]{1,0:T(8,128)}, f32[16,128]{1,0:T(8,128)S(1)}, u32[]{:S(2)}, u32[]{:S(2)}) collective-permute-start(f32[16,128]{1,0:T(8,128)} %lse_hbm.1), channel_id=1, source_target_pairs={{0,4},{4,0},{8,12},{12,8},{16,20},{20,16},{24,28},{28,24},{1,5},{5... | collective-permute-start | bytes 24584 | tf_op jit(solution)/shard_map/ppermute | solution.py:126
  13.1 5.5 %collective-permute-start.7 = (f32[16,128]{1,0:T(8,128)S(1)}, f32[16,128]{1,0:T(8,128)S(1)}, u32[]{:S(2)}, u32[]{:S(2)}) collective-permute-start(f32[16,128]{1,0:T(8,128)S(1)} %get-tuple-element.18), channel_id=1, source_target_pairs={{0,8},{4,12},{8,0},{12,4},{16,24},{20,28},{24,16},{28,20},{1,9},{5... | collective-permute-start | bytes 24584 | tf_op jit(solution)/shard_map/ppermute | solution.py:126
  15.6 5.4 %collective-permute-start.4 = (f32[16,128]{1,0:T(8,128)S(1)}, f32[16,128]{1,0:T(8,128)S(1)}, u32[]{:S(2)}, u32[]{:S(2)}) collective-permute-start(f32[16,128]{1,0:T(8,128)S(1)} %shard_map.48), channel_id=1, source_target_pairs={{0,24},{4,28},{8,16},{12,20},{16,8},{20,12},{24,0},{28,4},{1,25},{... | collective-permute-start | bytes 24584 | tf_op jit(solution)/shard_map/ppermute | solution.py:126
  18.1 4.6 %collective-permute-start.6 = (f32[16,128]{1,0:T(8,128)S(1)}, f32[16,128]{1,0:T(8,128)S(1)}, u32[]{:S(2)}, u32[]{:S(2)}) collective-permute-start(f32[16,128]{1,0:T(8,128)S(1)} %shard_map.49), channel_id=1, source_target_pairs={{0,16},{4,20},{8,24},{12,28},{16,0},{20,4},{24,8},{28,12},{1,17},{... | collective-permute-start | bytes 24584 | tf_op jit(solution)/shard_map/ppermute | solution.py:126

commit v2 on v1

v2 whole, which is shorter than its diff:
```python
import functools

import jax
import jax.numpy as jnp
from jax import lax
from jax.experimental import pallas as pl
from jax.experimental.pallas import tpu as pltpu
from jax.sharding import PartitionSpec as P


HEAD_DIM = 64
LANES = 128
LOG2E = 1.4426950408889634
MASKED = 1e30
VMEM_BYTES = 12 * 1024 * 1024
PIECES = 3


def offset_tile(lse_ref, block_index, limit):
    heads, rows = lse_ref.shape
    row = block_index * rows + lax.broadcasted_iota(jnp.int32, (heads, rows), 1)
    rest = jnp.where(row < limit, lse_ref[...], MASKED)
    pieces = []
    for _ in range(PIECES):
        piece = rest.astype(jnp.bfloat16).astype(jnp.float32)
        pieces.append(piece)
        rest = rest - piece
    pieces.append(jnp.zeros((LANES - PIECES * heads, rows), jnp.float32))
    return jnp.concatenate(pieces, axis=0).T.astype(jnp.bfloat16)


def add_block(key_ref, query_refs, offset_refs, out_ref, diagonal=False):
    width = key_ref.shape[0]
    heads = out_ref.shape[0]
    group = heads * HEAD_DIM // key_ref.shape[1]
    scale = HEAD_DIM ** (-0.5) * LOG2E
    low = lax.broadcasted_iota(jnp.int32, (width, LANES), 1) < HEAD_DIM
    lane = lax.broadcasted_iota(jnp.int32, (1, LANES), 1)
    offsets = jnp.concatenate([ref[...] for ref in offset_refs], axis=0)
    if diagonal:
        rows = query_refs[0].shape[0]
        causal = lax.broadcasted_iota(jnp.int32, (rows, width), 0) >= lax.broadcasted_iota(jnp.int32, (rows, width), 1)

    def picked(head):
        hit = lane == head
        for piece in range(1, PIECES):
            hit |= lane == piece * heads + head
        return jnp.broadcast_to(jnp.where(hit, -(HEAD_DIM**0.5), 0.0).astype(jnp.bfloat16), (width, LANES))

    for tile in range(key_ref.shape[1] // LANES):
        straight = key_ref[:, tile * LANES : (tile + 1) * LANES].astype(jnp.float32)
        swapped = pltpu.roll(straight, HEAD_DIM, 1)
        for half in range(LANES // HEAD_DIM):
            left, right = (straight, swapped) if half == 0 else (swapped, straight)
            spread = [jnp.where(low, left, 0.0).astype(jnp.bfloat16), jnp.where(low, 0.0, right).astype(jnp.bfloat16)]
            first_head = (2 * tile + half) * group
            for head in range(first_head, first_head + group, 2):
                lanes = slice(head * HEAD_DIM, (head + 2) * HEAD_DIM)
                deep = jnp.concatenate([ref[:, lanes] for ref in query_refs], axis=0)
                logits = lax.dot_general(
                    jnp.concatenate([deep, offsets], axis=1),
                    jnp.concatenate(
                        [jnp.concatenate([spread[side], picked(head + side)], axis=1) for side in range(2)], axis=0
                    ),
                    (((1,), (1,)), ((), ())),
                    preferred_element_type=jnp.float32,
                )
                for side in range(2):
                    weights = jnp.exp2(logits[:, side * width : (side + 1) * width] * scale)
                    if diagonal:
                        weights = jnp.where(causal, weights, 0.0)
                    out_ref[head + side : head + side + 1, :] += jnp.sum(weights, axis=0, keepdims=True)


def local_kernel(length_ref, lse_hbm, query_hbm, key_hbm, own_ref, offset_ref, query_ref, key_ref, lse_ref, sems):
    copies = [
        pltpu.make_async_copy(source, target, sems.at[at])
        for at, (source, target) in enumerate([(lse_hbm, lse_ref), (key_hbm, key_ref), (query_hbm, query_ref)])
    ]
    for copy in copies:
        copy.start()
    copies[0].wait()
    offset_ref[...] = offset_tile(lse_ref, lax.axis_index("ctx"), length_ref[0])
    own_ref[...] = jnp.zeros_like(own_ref)
    copies[1].wait()
    copies[2].wait()
    add_block(key_ref, [query_ref], [offset_ref], own_ref, diagonal=True)


def pair_kernel(xor, query_ref, query_1_ref, offset_ref, offset_1_ref, key_ref, out_ref):
    me = lax.axis_index("ctx")
    out_ref[...] = jnp.zeros_like(out_ref)

    @pl.when((me ^ xor) < me)
    def _():
        add_block(key_ref, [query_ref, query_1_ref], [offset_ref, offset_1_ref], out_ref)


def first_kernel(xor, length_ref, query_ref, query_1_ref, offset_ref, lse_1_ref, key_ref, out_ref, offset_1_ref):
    offset_1_ref[...] = offset_tile(lse_1_ref, lax.axis_index("ctx") ^ 1, length_ref[0])
    pair_kernel(xor, query_ref, query_1_ref, offset_ref, offset_1_ref, key_ref, out_ref)


def near_kernel(xor, query_ref, query_1_ref, offset_ref, offset_1_ref, key_x_ref, own_in_ref, key_ref, out_ref, own_ref):
    me = lax.axis_index("ctx")
    pair_kernel(xor, query_ref, query_1_ref, offset_ref, offset_1_ref, key_x_ref, out_ref)
    own_ref[...] = own_in_ref[...]

    @pl.when((me ^ 1) > me)
    def _():
        add_block(key_ref, [query_1_ref], [offset_1_ref], own_ref)


def call(body, out_shapes, operands, pairs, in_specs=None, scratch=()):
    heads, rows, width = out_shapes[0].shape[0], operands[-1].shape[0], LANES
    vmem = pl.BlockSpec(memory_space=pltpu.VMEM)
    return pl.pallas_call(
        body,
        out_shape=out_shapes,
        in_specs=in_specs or [vmem] * len(operands),
        out_specs=[vmem] * len(out_shapes),
        scratch_shapes=scratch,
        cost_estimate=pl.CostEstimate(
            flops=2 * pairs * heads * rows * width * HEAD_DIM,
            bytes_accessed=sum(x.size * x.dtype.itemsize for x in operands),
            transcendentals=pairs * heads * rows * width,
        ),
        compiler_params=pltpu.CompilerParams(vmem_limit_bytes=VMEM_BYTES),
    )(*operands)


def far_xors(devices_ctx):
    return list(range(devices_ctx - 2, 2, -2))


def shards(queries, keys, lse, length):
    devices_ctx = lax.axis_size("ctx")
    heads, rows = lse.shape
    sums = jax.ShapeDtypeStruct((heads, keys.shape[0]), jnp.float32)
    offsets = jax.ShapeDtypeStruct((rows, LANES), jnp.bfloat16)

    def swap(x, bit):
        return lax.ppermute(x, "ctx", [(i, i ^ bit) for i in range(devices_ctx)])

    xors = far_xors(devices_ctx)
    lse_1 = swap(lse, 1)
    queries_1 = swap(queries, 1)
    keys_x = {x: swap(keys, x) for x in xors + [2]}

    hbm, vmem, smem = (pl.BlockSpec(memory_space=space) for space in (pltpu.HBM, pltpu.VMEM, pltpu.SMEM))
    own, offset, queries, keys = call(
        local_kernel,
        [sums, offsets, queries, keys],
        [length] + [pltpu.with_memory_space_constraint(x, pltpu.HBM) for x in (lse, queries, keys)],
        1,
        [smem, hbm, hbm, hbm],
        [pltpu.VMEM(lse.shape, lse.dtype), pltpu.SemaphoreType.DMA((3,))],
    )
    back = []
    for x in xors:
        if not back:
            part, offset_1 = call(
                functools.partial(first_kernel, x),
                [sums, offsets],
                [length, queries, queries_1, offset, lse_1, keys_x[x]],
                2,
                [smem] + [vmem] * 5,
            )
            both = [queries, queries_1, offset, offset_1]
        else:
            (part,) = call(functools.partial(pair_kernel, x), [sums], both + [keys_x[x]], 2)
        back.append(swap(part, x))
    part, own = call(functools.partial(near_kernel, 2), [sums, sums], both + [keys_x[2], own, keys], 3)
    back.append(swap(part, 2))
    for term in back:
        own = own + term
    return own


def solution(mesh):
    placed = (P(("req", "ctx"), None), P(("req", "ctx"), None), P(None, ("req", "ctx")), P("req"))

    return jax.shard_map(shards, mesh=mesh, in_specs=placed, out_specs=P(None, ("req", "ctx")), check_vma=False)
```

time: 23.5 us -> 24 us (1.021)
  starting transfers between devices: 13.1 us -> 13.5 us
    ppermute x8, starting transfers between devices: 13.1 us -> 13.5 us  [swap(): return lax.ppermute(x, 'ctx', [(i, i ^ bit) for i in range(devices_ctx)])]
  transfers between devices with their start and end apart: 8 -> 8, of which waited for: 3 -> 4; matrix products, arithmetic and copies ran while one was open for 0% -> 0% of each run, Pallas kernels for 9% -> 9%
where the time goes in v2:
time: 24 us; the launch traced here: 23.8 us
  starting transfers between devices  13.5 us (56%)
  waiting for transfers between devices  6.87 us (29%)
  Pallas kernels  2.2 us (9%)
  between operations  0.68 us (3%)
  other arithmetic  0.6 us (2%)
    ppermute x8, starting transfers between devices, swap(): return lax.ppermute(x, 'ctx', [(i, i ^ bit) for i in range(devices_ctx)])  13.5 us
    ppermute x8, waiting for transfers between devices, swap(): return lax.ppermute(x, 'ctx', [(i, i ^ bit) for i in range(devices_ctx)])  6.87 us
    pallas_call x4, Pallas kernels, call(): pl.pallas_call(body, out_shape=out_shapes, in_specs=in_specs or [vmem] *...  2.2 us
    add x1, other arithmetic, shards(): own = own + term  0.6 us
  transfers between devices with their start and end apart: 8, of which 4 were waited for; matrix products, arithmetic and copies ran while one was open for 0% of the time, Pallas kernels for 9%

profile of v2, /device:TPU:0, one launch (start us, length us, event | category | flops | bytes accessed | tf_op | source)
XLA Modules:
  0.0 23.8 jit_solution(15193458744562065246)
XLA Ops:
  0.0 3.0 %collective-permute-start = (bf16[128,1024]{1,0:T(8,128)(2,1)}, bf16[128,1024]{1,0:T(8,128)(2,1)S(1)}, u32[]{:S(2)}, u32[]{:S(2)}) collective-permute-start(bf16[128,1024]{1,0:T(8,128)(2,1)} %query_hbm.1), channel_id=1, source_target_pairs={{0,4},{4,0},{8,12},{12,8},{16,20},{20,16},{24,28},{28,24},{1,5},{5... | collective-permute-start | bytes 786440 | tf_op jit(solution)/shard_map/ppermute | solution.py:143
  3.0 3.6 %collective-permute-start.2 = (bf16[128,256]{1,0:T(8,128)(2,1)}, bf16[128,256]{1,0:T(8,128)(2,1)S(1)}, u32[]{:S(2)}, u32[]{:S(2)}) collective-permute-start(bf16[128,256]{1,0:T(8,128)(2,1)} %key_hbm.1), channel_id=1, source_target_pairs={{0,24},{4,28},{8,16},{12,20},{16,8},{20,12},{24,0},{28,4},{1,25},{... | collective-permute-start | bytes 196616 | tf_op jit(solution)/shard_map/ppermute | solution.py:143
  6.6 0.0 collective-permute-start.3
  6.6 0.8 %collective-permute-start.5 = (bf16[128,256]{1,0:T(8,128)(2,1)}, bf16[128,256]{1,0:T(8,128)(2,1)S(1)}, u32[]{:S(2)}, u32[]{:S(2)}) collective-permute-start(bf16[128,256]{1,0:T(8,128)(2,1)} %key_hbm.1), channel_id=1, source_target_pairs={{0,16},{4,20},{8,24},{12,28},{16,0},{20,4},{24,8},{28,12},{1,17},{... | collective-permute-start | bytes 196616 | tf_op jit(solution)/shard_map/ppermute | solution.py:143
  7.4 0.3 %collective-permute-start.1 = (f32[16,128]{1,0:T(8,128)}, f32[16,128]{1,0:T(8,128)S(1)}, u32[]{:S(2)}, u32[]{:S(2)}) collective-permute-start(f32[16,128]{1,0:T(8,128)} %lse_hbm.1), channel_id=1, source_target_pairs={{0,4},{4,0},{8,12},{12,8},{16,20},{20,16},{24,28},{28,24},{1,5},{5... | collective-permute-start | bytes 24584 | tf_op jit(solution)/shard_map/ppermute | solution.py:143
  8.3 1.6 %shard_map.46 = (f32[16,128]{1,0:T(8,128)S(1)}, bf16[128,128]{1,0:T(8,128)(2,1)S(1)}, bf16[128,1024]{1,0:T(8,128)(2,1)S(1)}, bf16[128,256]{1,0:T(8,128)(2,1)S(1)}) custom-call(s32[1]{0:T(128)S(6)} %copy.5.length_ref, f32[16,128]{1,0:T(8,128)} %lse_hbm.1, bf16[128,1024]{1,0:T(8,128)(2,1)} %query_hbm.1, bf16[128,256]{1,0:T(8,128)(2,1)} %key_hbm.1), custom_call_target="tpu_custom_call" | custom-call | flops 33554432 | bytes 335876 | tf_op jit(solution)/shard_map/pallas_call | solution.py:117
  9.9 1.3 %collective-permute-done.1.lse_1_ref = f32[16,128]{1,0:T(8,128)S(1)} collective-permute-done((f32[16,128]{1,0:T(8,128)}, f32[16,128]{1,0:T(8,128)S(1)}, u32[]{:S(2)}, u32[]{:S(2)}) %collective-permute-start.1) | collective-permute-done | bytes 8224 | tf_op jit(solution)/shard_map/ppermute | solution.py:143
  11.2 0.0 collective-permute-done.2.key_ref
  11.3 0.0 collective-permute-done.query_1_ref
  11.3 0.1 shard_map.47
  11.4 0.1 collective-permute-done.3.key_x_ref
  11.4 0.5 %shard_map.48 = (f32[16,128]{1,0:T(8,128)S(1)}, f32[16,128]{1,0:T(8,128)S(1)}) custom-call(bf16[128,1024]{1,0:T(8,128)(2,1)S(1)} %get-tuple-element.13.query_ref, bf16[128,1024]{1,0:T(8,128)(2,1)S(1)} %collective-permute-done.query_1_ref, bf16[128,128]{1,0:T(8,128)(2,1)S(1)} %get-tuple-element.14.offset_ref, ...), custom_call_target="tpu_custom_call" | custom-call | flops 100663296 | bytes 729088 | tf_op jit(solution)/shard_map/pallas_call | solution.py:117
  12.0 1.8 %collective-permute-start.7 = (f32[16,128]{1,0:T(8,128)S(1)}, f32[16,128]{1,0:T(8,128)S(1)}, u32[]{:S(2)}, u32[]{:S(2)}) collective-permute-start(f32[16,128]{1,0:T(8,128)S(1)} %get-tuple-element.20), channel_id=1, source_target_pairs={{0,8},{4,12},{8,0},{12,4},{16,24},{20,28},{24,16},{28,20},{1,9},{5... | collective-permute-start | bytes 24584 | tf_op jit(solution)/shard_map/ppermute | solution.py:143
  13.7 0.0 collective-permute-done.5.key_ref
  13.7 4.0 %collective-permute-start.6 = (f32[16,128]{1,0:T(8,128)S(1)}, f32[16,128]{1,0:T(8,128)S(1)}, u32[]{:S(2)}, u32[]{:S(2)}) collective-permute-start(f32[16,128]{1,0:T(8,128)S(1)} %shard_map.49), channel_id=1, source_target_pairs={{0,16},{4,20},{8,24},{12,28},{16,0},{20,4},{24,8},{28,12},{1,17},{... | collective-permute-start | bytes 24584 | tf_op jit(solution)/shard_map/ppermute | solution.py:143
  17.8 0.0 collective-permute-start.4
  17.8 0.0 collective-permute-done.7
  17.8 1.6 %collective-permute-done.6 = f32[16,128]{1,0:T(8,128)S(1)} collective-permute-done((f32[16,128]{1,0:T(8,128)S(1)}, f32[16,128]{1,0:T(8,128)S(1)}, u32[]{:S(2)}, u32[]{:S(2)}) %collective-permute-start.6) | collective-permute-done | bytes 8224 | tf_op jit(solution)/shard_map/ppermute | solution.py:143
  19.4 3.8 %collective-permute-done.4 = f32[16,128]{1,0:T(8,128)S(1)} collective-permute-done((f32[16,128]{1,0:T(8,128)S(1)}, f32[16,128]{1,0:T(8,128)S(1)}, u32[]{:S(2)}, u32[]{:S(2)}) %collective-permute-start.4) | collective-permute-done | bytes 8224 | tf_op jit(solution)/shard_map/ppermute | solution.py:143
  23.2 0.6 %add_add_fusion = f32[16,128]{1,0:T(8,128)} fusion(f32[16,128]{1,0:T(8,128)S(1)} %collective-permute-done.7, f32[16,128]{1,0:T(8,128)S(1)} %collective-permute-done.6, f32[16,128]{1,0:T(8,128)S(1)} %get-tuple-element.18, f32[16,128]{1,0:T(8,128)S(1)} %collective-permute-done.4), kind=kLoop, calls=%fused_computation | loop fusion | flops 6144 | bytes 40960 | tf_op jit(solution)/shard_map/add | solution.py:176
  (1 shorter events, 0.0 us)
Async XLA Ops:
  0.0 11.3 %collective-permute-start = (bf16[128,1024]{1,0:T(8,128)(2,1)}, bf16[128,1024]{1,0:T(8,128)(2,1)S(1)}, u32[]{:S(2)}, u32[]{:S(2)}) collective-permute-start(bf16[128,1024]{1,0:T(8,128)(2,1)} %query_hbm.1), channel_id=1, source_target_pairs={{0,4},{4,0},{8,12},{12,8},{16,20},{20,16},{24,28},{28,24},{1,5},{5... | collective-permute-start | bytes 786440 | tf_op jit(solution)/shard_map/ppermute | solution.py:143
  3.0 8.3 %collective-permute-start.2 = (bf16[128,256]{1,0:T(8,128)(2,1)}, bf16[128,256]{1,0:T(8,128)(2,1)S(1)}, u32[]{:S(2)}, u32[]{:S(2)}) collective-permute-start(bf16[128,256]{1,0:T(8,128)(2,1)} %key_hbm.1), channel_id=1, source_target_pairs={{0,24},{4,28},{8,16},{12,20},{16,8},{20,12},{24,0},{28,4},{1,25},{... | collective-permute-start | bytes 196616 | tf_op jit(solution)/shard_map/ppermute | solution.py:143
  6.6 4.8 %collective-permute-start.3 = (bf16[128,256]{1,0:T(8,128)(2,1)}, bf16[128,256]{1,0:T(8,128)(2,1)S(1)}, u32[]{:S(2)}, u32[]{:S(2)}) collective-permute-start(bf16[128,256]{1,0:T(8,128)(2,1)} %key_hbm.1), channel_id=1, source_target_pairs={{0,8},{4,12},{8,0},{12,4},{16,24},{20,28},{24,16},{28,20},{1,9},{5... | collective-permute-start | bytes 196616 | tf_op jit(solution)/shard_map/ppermute | solution.py:143
  6.6 7.1 %collective-permute-start.5 = (bf16[128,256]{1,0:T(8,128)(2,1)}, bf16[128,256]{1,0:T(8,128)(2,1)S(1)}, u32[]{:S(2)}, u32[]{:S(2)}) collective-permute-start(bf16[128,256]{1,0:T(8,128)(2,1)} %key_hbm.1), channel_id=1, source_target_pairs={{0,16},{4,20},{8,24},{12,28},{16,0},{20,4},{24,8},{28,12},{1,17},{... | collective-permute-start | bytes 196616 | tf_op jit(solution)/shard_map/ppermute | solution.py:143
  7.4 3.9 %collective-permute-start.1 = (f32[16,128]{1,0:T(8,128)}, f32[16,128]{1,0:T(8,128)S(1)}, u32[]{:S(2)}, u32[]{:S(2)}) collective-permute-start(f32[16,128]{1,0:T(8,128)} %lse_hbm.1), channel_id=1, source_target_pairs={{0,4},{4,0},{8,12},{12,8},{16,20},{20,16},{24,28},{28,24},{1,5},{5... | collective-permute-start | bytes 24584 | tf_op jit(solution)/shard_map/ppermute | solution.py:143
  12.0 5.8 %collective-permute-start.7 = (f32[16,128]{1,0:T(8,128)S(1)}, f32[16,128]{1,0:T(8,128)S(1)}, u32[]{:S(2)}, u32[]{:S(2)}) collective-permute-start(f32[16,128]{1,0:T(8,128)S(1)} %get-tuple-element.20), channel_id=1, source_target_pairs={{0,8},{4,12},{8,0},{12,4},{16,24},{20,28},{24,16},{28,20},{1,9},{5... | collective-permute-start | bytes 24584 | tf_op jit(solution)/shard_map/ppermute | solution.py:143
  13.7 5.7 %collective-permute-start.6 = (f32[16,128]{1,0:T(8,128)S(1)}, f32[16,128]{1,0:T(8,128)S(1)}, u32[]{:S(2)}, u32[]{:S(2)}) collective-permute-start(f32[16,128]{1,0:T(8,128)S(1)} %shard_map.49), channel_id=1, source_target_pairs={{0,16},{4,20},{8,24},{12,28},{16,0},{20,4},{24,8},{28,12},{1,17},{... | collective-permute-start | bytes 24584 | tf_op jit(solution)/shard_map/ppermute | solution.py:143
  17.8 5.4 %collective-permute-start.4 = (f32[16,128]{1,0:T(8,128)S(1)}, f32[16,128]{1,0:T(8,128)S(1)}, u32[]{:S(2)}, u32[]{:S(2)}) collective-permute-start(f32[16,128]{1,0:T(8,128)S(1)} %get-tuple-element.19), channel_id=1, source_target_pairs={{0,24},{4,28},{8,16},{12,20},{16,8},{20,12},{24,0},{28,4},{1,25},{... | collective-permute-start | bytes 24584 | tf_op jit(solution)/shard_map/ppermute | solution.py:143

commit v3 on v2

--- a/solution.py
+++ b/solution.py
@@ -101,9 +101,8 @@
     pair_kernel(xor, query_ref, query_1_ref, offset_ref, offset_1_ref, key_ref, out_ref)
 
 
-def near_kernel(xor, query_ref, query_1_ref, offset_ref, offset_1_ref, key_x_ref, own_in_ref, key_ref, out_ref, own_ref):
+def partner_kernel(query_1_ref, offset_1_ref, key_ref, own_in_ref, own_ref):
     me = lax.axis_index("ctx")
-    pair_kernel(xor, query_ref, query_1_ref, offset_ref, offset_1_ref, key_x_ref, out_ref)
     own_ref[...] = own_in_ref[...]
 
     @pl.when((me ^ 1) > me)
@@ -139,8 +138,9 @@
     sums = jax.ShapeDtypeStruct((heads, keys.shape[0]), jnp.float32)
     offsets = jax.ShapeDtypeStruct((rows, LANES), jnp.bfloat16)
 
-    def swap(x, bit):
-        return lax.ppermute(x, "ctx", [(i, i ^ bit) for i in range(devices_ctx)])
+    def swap(x, bit, up=None):
+        pairs = [(i, i ^ bit if up is None or i ^ bit < i else i ^ up) for i in range(devices_ctx)]
+        return lax.ppermute(x, "ctx", pairs)
 
     xors = far_xors(devices_ctx)
     lse_1 = swap(lse, 1)
@@ -169,9 +169,10 @@
             both = [queries, queries_1, offset, offset_1]
         else:
             (part,) = call(functools.partial(pair_kernel, x), [sums], both + [keys_x[x]], 2)
-        back.append(swap(part, x))
-    part, own = call(functools.partial(near_kernel, 2), [sums, sums], both + [keys_x[2], own, keys], 3)
+        back.append(swap(part, x, up=1 << (x.bit_length() - 1)))
+    (part,) = call(functools.partial(pair_kernel, 2), [sums], both + [keys_x[2]], 2)
     back.append(swap(part, 2))
+    (own,) = call(partner_kernel, [sums], [queries_1, offset_1, keys, own], 1)
     for term in back:
         own = own + term
     return own

time: 24 us -> 23.5 us (0.979)
  starting transfers between devices: 13.5 us -> 12.7 us
    ppermute x8, starting transfers between devices: 13.5 us -> 12.7 us  [swap(): return lax.ppermute(x, 'ctx', pairs)]
    pallas_call x4 -> x5, Pallas kernels: 2.2 us -> 2.2 us  [call(): pl.pallas_call(body, out_shape=out_shapes, in_specs=in_specs or [vmem] *...]
where the time goes in v3:
time: 23.5 us; the launch traced here: 23.3 us
  starting transfers between devices  12.7 us (54%)
  waiting for transfers between devices  7.1 us (30%)
  Pallas kernels  2.2 us (9%)
  between operations  0.69 us (3%)
  other arithmetic  0.6 us (3%)
    ppermute x8, starting transfers between devices, swap(): return lax.ppermute(x, 'ctx', pairs)  12.7 us
    ppermute x8, waiting for transfers between devices, swap(): return lax.ppermute(x, 'ctx', pairs)  7.1 us
    pallas_call x5, Pallas kernels, call(): pl.pallas_call(body, out_shape=out_shapes, in_specs=in_specs or [vmem] *...  2.2 us
    add x1, other arithmetic, shards(): own = own + term  0.6 us
  transfers between devices with their start and end apart: 8, of which 4 were waited for; matrix products, arithmetic and copies ran while one was open for 0% of the time, Pallas kernels for 9%

profile of v3, /device:TPU:0, one launch (start us, length us, event | category | flops | bytes accessed | tf_op | source)
XLA Modules:
  0.0 23.3 jit_solution(15337610300034450386)
XLA Ops:
  0.0 3.0 %collective-permute-start = (bf16[128,1024]{1,0:T(8,128)(2,1)}, bf16[128,1024]{1,0:T(8,128)(2,1)S(1)}, u32[]{:S(2)}, u32[]{:S(2)}) collective-permute-start(bf16[128,1024]{1,0:T(8,128)(2,1)} %query_hbm.1), channel_id=1, source_target_pairs={{0,4},{4,0},{8,12},{12,8},{16,20},{20,16},{24,28},{28,24},{1,5},{5... | collective-permute-start | bytes 786440 | tf_op jit(solution)/shard_map/ppermute | solution.py:143
  3.0 3.6 %collective-permute-start.2 = (bf16[128,256]{1,0:T(8,128)(2,1)}, bf16[128,256]{1,0:T(8,128)(2,1)S(1)}, u32[]{:S(2)}, u32[]{:S(2)}) collective-permute-start(bf16[128,256]{1,0:T(8,128)(2,1)} %key_hbm.1), channel_id=1, source_target_pairs={{0,24},{4,28},{8,16},{12,20},{16,8},{20,12},{24,0},{28,4},{1,25},{... | collective-permute-start | bytes 196616 | tf_op jit(solution)/shard_map/ppermute | solution.py:143
  6.6 0.0 collective-permute-start.4
  6.6 0.8 %collective-permute-start.6 = (bf16[128,256]{1,0:T(8,128)(2,1)}, bf16[128,256]{1,0:T(8,128)(2,1)S(1)}, u32[]{:S(2)}, u32[]{:S(2)}) collective-permute-start(bf16[128,256]{1,0:T(8,128)(2,1)} %key_hbm.1), channel_id=1, source_target_pairs={{0,8},{4,12},{8,0},{12,4},{16,24},{20,28},{24,16},{28,20},{1,9},{5... | collective-permute-start | bytes 196616 | tf_op jit(solution)/shard_map/ppermute | solution.py:143
  7.4 0.3 %collective-permute-start.1 = (f32[16,128]{1,0:T(8,128)}, f32[16,128]{1,0:T(8,128)S(1)}, u32[]{:S(2)}, u32[]{:S(2)}) collective-permute-start(f32[16,128]{1,0:T(8,128)} %lse_hbm.1), channel_id=1, source_target_pairs={{0,4},{4,0},{8,12},{12,8},{16,20},{20,16},{24,28},{28,24},{1,5},{5... | collective-permute-start | bytes 24584 | tf_op jit(solution)/shard_map/ppermute | solution.py:143
  8.3 1.6 %shard_map.46 = (f32[16,128]{1,0:T(8,128)S(1)}, bf16[128,128]{1,0:T(8,128)(2,1)S(1)}, bf16[128,1024]{1,0:T(8,128)(2,1)S(1)}, bf16[128,256]{1,0:T(8,128)(2,1)S(1)}) custom-call(s32[1]{0:T(128)S(6)} %copy.5.length_ref, f32[16,128]{1,0:T(8,128)} %lse_hbm.1, bf16[128,1024]{1,0:T(8,128)(2,1)} %query_hbm.1, bf16[128,256]{1,0:T(8,128)(2,1)} %key_hbm.1), custom_call_target="tpu_custom_call" | custom-call | flops 33554432 | bytes 335876 | tf_op jit(solution)/shard_map/pallas_call | solution.py:116
  9.9 1.3 %collective-permute-done.1.lse_1_ref = f32[16,128]{1,0:T(8,128)S(1)} collective-permute-done((f32[16,128]{1,0:T(8,128)}, f32[16,128]{1,0:T(8,128)S(1)}, u32[]{:S(2)}, u32[]{:S(2)}) %collective-permute-start.1) | collective-permute-done | bytes 8224 | tf_op jit(solution)/shard_map/ppermute | solution.py:143
  11.2 0.0 collective-permute-done.2.key_ref
  11.3 0.0 collective-permute-done.query_1_ref
  11.3 0.1 shard_map.47
  11.4 0.9 %collective-permute-done.4.key_ref = bf16[128,256]{1,0:T(8,128)(2,1)S(1)} collective-permute-done((bf16[128,256]{1,0:T(8,128)(2,1)}, bf16[128,256]{1,0:T(8,128)(2,1)S(1)}, u32[]{:S(2)}, u32[]{:S(2)}) %collective-permute-start.4) | collective-permute-done | bytes 65568 | tf_op jit(solution)/shard_map/ppermute | solution.py:143
  12.2 2.4 %collective-permute-start.5 = (f32[16,128]{1,0:T(8,128)S(1)}, f32[16,128]{1,0:T(8,128)S(1)}, u32[]{:S(2)}, u32[]{:S(2)}) collective-permute-start(f32[16,128]{1,0:T(8,128)S(1)} %shard_map.49), channel_id=1, source_target_pairs={{0,16},{4,20},{8,24},{12,28},{16,0},{20,4},{24,8},{28,12},{1,17},{... | collective-permute-start | bytes 24584 | tf_op jit(solution)/shard_map/ppermute | solution.py:143
  14.6 0.0 collective-permute-done.6.key_ref
  14.6 2.6 %collective-permute-start.7 = (f32[16,128]{1,0:T(8,128)S(1)}, f32[16,128]{1,0:T(8,128)S(1)}, u32[]{:S(2)}, u32[]{:S(2)}) collective-permute-start(f32[16,128]{1,0:T(8,128)S(1)} %shard_map.50), channel_id=1, source_target_pairs={{0,8},{4,12},{8,0},{12,4},{16,24},{20,28},{24,16},{28,20},{1,9},{5... | collective-permute-start | bytes 24584 | tf_op jit(solution)/shard_map/ppermute | solution.py:143
  17.2 0.0 collective-permute-start.3
  17.3 0.5 %shard_map.48 = f32[16,128]{1,0:T(8,128)S(1)} custom-call(bf16[128,1024]{1,0:T(8,128)(2,1)S(1)} %collective-permute-done.query_1_ref, bf16[128,128]{1,0:T(8,128)(2,1)S(1)} %get-tuple-element.13.offset_1_ref, bf16[128,256]{1,0:T(8,128)(2,1)S(1)} %get-tuple-element.14.key_ref, f32[16,128]{1,0:T(8,128)S(1)} %get-tuple-element.15.own_in_ref), custom_call_target="tpu_custom_call" | custom-call | flops 4194304 | bytes 368640 | tf_op jit(solution)/shard_map/pallas_call | solution.py:116
  17.8 0.0 collective-permute-done.5
  17.8 1.1 %collective-permute-done.7 = f32[16,128]{1,0:T(8,128)S(1)} collective-permute-done((f32[16,128]{1,0:T(8,128)S(1)}, f32[16,128]{1,0:T(8,128)S(1)}, u32[]{:S(2)}, u32[]{:S(2)}) %collective-permute-start.7) | collective-permute-done | bytes 8224 | tf_op jit(solution)/shard_map/ppermute | solution.py:143
  18.9 3.8 %collective-permute-done.3 = f32[16,128]{1,0:T(8,128)S(1)} collective-permute-done((f32[16,128]{1,0:T(8,128)S(1)}, f32[16,128]{1,0:T(8,128)S(1)}, u32[]{:S(2)}, u32[]{:S(2)}) %collective-permute-start.3) | collective-permute-done | bytes 8224 | tf_op jit(solution)/shard_map/ppermute | solution.py:143
  22.7 0.6 %add_add_fusion = f32[16,128]{1,0:T(8,128)} fusion(f32[16,128]{1,0:T(8,128)S(1)} %collective-permute-done.7, f32[16,128]{1,0:T(8,128)S(1)} %collective-permute-done.5, f32[16,128]{1,0:T(8,128)S(1)} %shard_map.48, f32[16,128]{1,0:T(8,128)S(1)} %collective-permute-done.3), kind=kLoop, calls=%fused_computation | loop fusion | flops 6144 | bytes 40960 | tf_op jit(solution)/shard_map/add | solution.py:177
  (2 shorter events, 0.0 us)
Async XLA Ops:
  0.0 11.3 %collective-permute-start = (bf16[128,1024]{1,0:T(8,128)(2,1)}, bf16[128,1024]{1,0:T(8,128)(2,1)S(1)}, u32[]{:S(2)}, u32[]{:S(2)}) collective-permute-start(bf16[128,1024]{1,0:T(8,128)(2,1)} %query_hbm.1), channel_id=1, source_target_pairs={{0,4},{4,0},{8,12},{12,8},{16,20},{20,16},{24,28},{28,24},{1,5},{5... | collective-permute-start | bytes 786440 | tf_op jit(solution)/shard_map/ppermute | solution.py:143
  3.0 8.3 %collective-permute-start.2 = (bf16[128,256]{1,0:T(8,128)(2,1)}, bf16[128,256]{1,0:T(8,128)(2,1)S(1)}, u32[]{:S(2)}, u32[]{:S(2)}) collective-permute-start(bf16[128,256]{1,0:T(8,128)(2,1)} %key_hbm.1), channel_id=1, source_target_pairs={{0,24},{4,28},{8,16},{12,20},{16,8},{20,12},{24,0},{28,4},{1,25},{... | collective-permute-start | bytes 196616 | tf_op jit(solution)/shard_map/ppermute | solution.py:143
  6.6 5.6 %collective-permute-start.4 = (bf16[128,256]{1,0:T(8,128)(2,1)}, bf16[128,256]{1,0:T(8,128)(2,1)S(1)}, u32[]{:S(2)}, u32[]{:S(2)}) collective-permute-start(bf16[128,256]{1,0:T(8,128)(2,1)} %key_hbm.1), channel_id=1, source_target_pairs={{0,16},{4,20},{8,24},{12,28},{16,0},{20,4},{24,8},{28,12},{1,17},{... | collective-permute-start | bytes 196616 | tf_op jit(solution)/shard_map/ppermute | solution.py:143
  6.6 8.0 %collective-permute-start.6 = (bf16[128,256]{1,0:T(8,128)(2,1)}, bf16[128,256]{1,0:T(8,128)(2,1)S(1)}, u32[]{:S(2)}, u32[]{:S(2)}) collective-permute-start(bf16[128,256]{1,0:T(8,128)(2,1)} %key_hbm.1), channel_id=1, source_target_pairs={{0,8},{4,12},{8,0},{12,4},{16,24},{20,28},{24,16},{28,20},{1,9},{5... | collective-permute-start | bytes 196616 | tf_op jit(solution)/shard_map/ppermute | solution.py:143
  7.4 3.9 %collective-permute-start.1 = (f32[16,128]{1,0:T(8,128)}, f32[16,128]{1,0:T(8,128)S(1)}, u32[]{:S(2)}, u32[]{:S(2)}) collective-permute-start(f32[16,128]{1,0:T(8,128)} %lse_hbm.1), channel_id=1, source_target_pairs={{0,4},{4,0},{8,12},{12,8},{16,20},{20,16},{24,28},{28,24},{1,5},{5... | collective-permute-start | bytes 24584 | tf_op jit(solution)/shard_map/ppermute | solution.py:143
  12.2 5.6 %collective-permute-start.5 = (f32[16,128]{1,0:T(8,128)S(1)}, f32[16,128]{1,0:T(8,128)S(1)}, u32[]{:S(2)}, u32[]{:S(2)}) collective-permute-start(f32[16,128]{1,0:T(8,128)S(1)} %shard_map.49), channel_id=1, source_target_pairs={{0,16},{4,20},{8,24},{12,28},{16,0},{20,4},{24,8},{28,12},{1,17},{... | collective-permute-start | bytes 24584 | tf_op jit(solution)/shard_map/ppermute | solution.py:143
  14.6 4.3 %collective-permute-start.7 = (f32[16,128]{1,0:T(8,128)S(1)}, f32[16,128]{1,0:T(8,128)S(1)}, u32[]{:S(2)}, u32[]{:S(2)}) collective-permute-start(f32[16,128]{1,0:T(8,128)S(1)} %shard_map.50), channel_id=1, source_target_pairs={{0,8},{4,12},{8,0},{12,4},{16,24},{20,28},{24,16},{28,20},{1,9},{5... | collective-permute-start | bytes 24584 | tf_op jit(solution)/shard_map/ppermute | solution.py:143
  17.2 5.4 %collective-permute-start.3 = (f32[16,128]{1,0:T(8,128)S(1)}, f32[16,128]{1,0:T(8,128)S(1)}, u32[]{:S(2)}, u32[]{:S(2)}) collective-permute-start(f32[16,128]{1,0:T(8,128)S(1)} %get-tuple-element.16), channel_id=1, source_target_pairs={{0,16},{4,20},{8,24},{12,28},{16,8},{20,12},{24,0},{28,4},{1,17},{... | collective-permute-start | bytes 24584 | tf_op jit(solution)/shard_map/ppermute | solution.py:143

commit v4 on v3

--- a/solution.py
+++ b/solution.py
@@ -87,11 +87,15 @@
     add_block(key_ref, [query_ref], [offset_ref], own_ref, diagonal=True)
 
 
-def pair_kernel(xor, query_ref, query_1_ref, offset_ref, offset_1_ref, key_ref, out_ref):
+def pair_kernel(xor, query_ref, query_1_ref, offset_ref, offset_1_ref, key_ref, *refs, upper=None):
+    out_ref = refs[-1]
     me = lax.axis_index("ctx")
-    out_ref[...] = jnp.zeros_like(out_ref)
+    out_ref[...] = refs[0][...] if len(refs) > 1 else jnp.zeros_like(out_ref)
+    wanted = (me ^ xor) < me
+    if upper is not None:
+        wanted &= (me >= lax.axis_size("ctx") // 2) == upper
 
-    @pl.when((me ^ xor) < me)
+    @pl.when(wanted)
     def _():
         add_block(key_ref, [query_ref, query_1_ref], [offset_ref, offset_1_ref], out_ref)
 
@@ -129,6 +133,8 @@
 
 
 def far_xors(devices_ctx):
+    if devices_ctx < 8 or devices_ctx & (devices_ctx - 1):
+        raise ValueError(devices_ctx)
     return list(range(devices_ctx - 2, 2, -2))
 
 
@@ -170,7 +176,9 @@
         else:
             (part,) = call(functools.partial(pair_kernel, x), [sums], both + [keys_x[x]], 2)
         back.append(swap(part, x, up=1 << (x.bit_length() - 1)))
-    (part,) = call(functools.partial(pair_kernel, 2), [sums], both + [keys_x[2]], 2)
+    near = both + [keys_x[2]]
+    (part,) = call(functools.partial(pair_kernel, 2, upper=False), [sums], near, 2)
+    (part,) = call(functools.partial(pair_kernel, 2, upper=True), [sums], near + [part], 2)
     back.append(swap(part, 2))
     (own,) = call(partner_kernel, [sums], [queries_1, offset_1, keys, own], 1)
     for term in back:

time: 23.5 us -> 23.5 us (level)
    pallas_call x5 -> x6, Pallas kernels: 2.2 us -> 2.21 us  [call(): pl.pallas_call(body, out_shape=out_shapes, in_specs=in_specs or [vmem] *...]
where the time goes in v4:
time: 23.5 us; the launch traced here: 23.3 us
  starting transfers between devices  12.7 us (54%)
  waiting for transfers between devices  7.11 us (30%)
  Pallas kernels  2.21 us (9%)
  between operations  0.69 us (3%)
  other arithmetic  0.6 us (3%)
    ppermute x8, starting transfers between devices, swap(): return lax.ppermute(x, 'ctx', pairs)  12.7 us
    ppermute x8, waiting for transfers between devices, swap(): return lax.ppermute(x, 'ctx', pairs)  7.11 us
    pallas_call x6, Pallas kernels, call(): pl.pallas_call(body, out_shape=out_shapes, in_specs=in_specs or [vmem] *...  2.21 us
    add x1, other arithmetic, shards(): own = own + term  0.6 us
  transfers between devices with their start and end apart: 8, of which 4 were waited for; matrix products, arithmetic and copies ran while one was open for 0% of the time, Pallas kernels for 9%

profile of v4, /device:TPU:0, one launch (start us, length us, event | category | flops | bytes accessed | tf_op | source)
XLA Modules:
  0.0 23.3 jit_solution(11752806708598034196)
XLA Ops:
  0.0 3.0 %collective-permute-start = (bf16[128,1024]{1,0:T(8,128)(2,1)}, bf16[128,1024]{1,0:T(8,128)(2,1)S(1)}, u32[]{:S(2)}, u32[]{:S(2)}) collective-permute-start(bf16[128,1024]{1,0:T(8,128)(2,1)} %query_hbm.1), channel_id=1, source_target_pairs={{0,4},{4,0},{8,12},{12,8},{16,20},{20,16},{24,28},{28,24},{1,5},{5... | collective-permute-start | bytes 786440 | tf_op jit(solution)/shard_map/ppermute | solution.py:149
  3.0 3.6 %collective-permute-start.2 = (bf16[128,256]{1,0:T(8,128)(2,1)}, bf16[128,256]{1,0:T(8,128)(2,1)S(1)}, u32[]{:S(2)}, u32[]{:S(2)}) collective-permute-start(bf16[128,256]{1,0:T(8,128)(2,1)} %key_hbm.1), channel_id=1, source_target_pairs={{0,24},{4,28},{8,16},{12,20},{16,8},{20,12},{24,0},{28,4},{1,25},{... | collective-permute-start | bytes 196616 | tf_op jit(solution)/shard_map/ppermute | solution.py:149
  6.6 0.0 collective-permute-start.4
  6.6 0.8 %collective-permute-start.6 = (bf16[128,256]{1,0:T(8,128)(2,1)}, bf16[128,256]{1,0:T(8,128)(2,1)S(1)}, u32[]{:S(2)}, u32[]{:S(2)}) collective-permute-start(bf16[128,256]{1,0:T(8,128)(2,1)} %key_hbm.1), channel_id=1, source_target_pairs={{0,8},{4,12},{8,0},{12,4},{16,24},{20,28},{24,16},{28,20},{1,9},{5... | collective-permute-start | bytes 196616 | tf_op jit(solution)/shard_map/ppermute | solution.py:149
  7.4 0.3 %collective-permute-start.1 = (f32[16,128]{1,0:T(8,128)}, f32[16,128]{1,0:T(8,128)S(1)}, u32[]{:S(2)}, u32[]{:S(2)}) collective-permute-start(f32[16,128]{1,0:T(8,128)} %lse_hbm.1), channel_id=1, source_target_pairs={{0,4},{4,0},{8,12},{12,8},{16,20},{20,16},{24,28},{28,24},{1,5},{5... | collective-permute-start | bytes 24584 | tf_op jit(solution)/shard_map/ppermute | solution.py:149
  8.3 1.6 %shard_map.46 = (f32[16,128]{1,0:T(8,128)S(1)}, bf16[128,128]{1,0:T(8,128)(2,1)S(1)}, bf16[128,1024]{1,0:T(8,128)(2,1)S(1)}, bf16[128,256]{1,0:T(8,128)(2,1)S(1)}) custom-call(s32[1]{0:T(128)S(6)} %copy.5.length_ref, f32[16,128]{1,0:T(8,128)} %lse_hbm.1, bf16[128,1024]{1,0:T(8,128)(2,1)} %query_hbm.1, bf16[128,256]{1,0:T(8,128)(2,1)} %key_hbm.1), custom_call_target="tpu_custom_call" | custom-call | flops 33554432 | bytes 335876 | tf_op jit(solution)/shard_map/pallas_call | solution.py:120
  9.9 1.3 %collective-permute-done.1.lse_1_ref = f32[16,128]{1,0:T(8,128)S(1)} collective-permute-done((f32[16,128]{1,0:T(8,128)}, f32[16,128]{1,0:T(8,128)S(1)}, u32[]{:S(2)}, u32[]{:S(2)}) %collective-permute-start.1) | collective-permute-done | bytes 8224 | tf_op jit(solution)/shard_map/ppermute | solution.py:149
  11.2 0.0 collective-permute-done.2.key_ref
  11.3 0.0 collective-permute-done.query_1_ref
  11.3 0.1 shard_map.47
  11.4 0.9 %collective-permute-done.4.key_ref = bf16[128,256]{1,0:T(8,128)(2,1)S(1)} collective-permute-done((bf16[128,256]{1,0:T(8,128)(2,1)}, bf16[128,256]{1,0:T(8,128)(2,1)S(1)}, u32[]{:S(2)}, u32[]{:S(2)}) %collective-permute-start.4) | collective-permute-done | bytes 65568 | tf_op jit(solution)/shard_map/ppermute | solution.py:149
  12.2 2.4 %collective-permute-start.5 = (f32[16,128]{1,0:T(8,128)S(1)}, f32[16,128]{1,0:T(8,128)S(1)}, u32[]{:S(2)}, u32[]{:S(2)}) collective-permute-start(f32[16,128]{1,0:T(8,128)S(1)} %shard_map.49), channel_id=1, source_target_pairs={{0,16},{4,20},{8,24},{12,28},{16,0},{20,4},{24,8},{28,12},{1,17},{... | collective-permute-start | bytes 24584 | tf_op jit(solution)/shard_map/ppermute | solution.py:149
  14.6 0.0 collective-permute-done.6.key_ref
  14.6 2.6 %collective-permute-start.7 = (f32[16,128]{1,0:T(8,128)S(1)}, f32[16,128]{1,0:T(8,128)S(1)}, u32[]{:S(2)}, u32[]{:S(2)}) collective-permute-start(f32[16,128]{1,0:T(8,128)S(1)} %shard_map.51), channel_id=1, source_target_pairs={{0,8},{4,12},{8,0},{12,4},{16,24},{20,28},{24,16},{28,20},{1,9},{5... | collective-permute-start | bytes 24584 | tf_op jit(solution)/shard_map/ppermute | solution.py:149
  17.3 0.0 collective-permute-start.3
  17.3 0.5 %shard_map.48 = f32[16,128]{1,0:T(8,128)S(1)} custom-call(bf16[128,1024]{1,0:T(8,128)(2,1)S(1)} %collective-permute-done.query_1_ref, bf16[128,128]{1,0:T(8,128)(2,1)S(1)} %get-tuple-element.13.offset_1_ref, bf16[128,256]{1,0:T(8,128)(2,1)S(1)} %get-tuple-element.14.key_ref, f32[16,128]{1,0:T(8,128)S(1)} %get-tuple-element.15.own_in_ref), custom_call_target="tpu_custom_call" | custom-call | flops 4194304 | bytes 368640 | tf_op jit(solution)/shard_map/pallas_call | solution.py:120
  17.8 0.0 collective-permute-done.5
  17.8 1.1 %collective-permute-done.7 = f32[16,128]{1,0:T(8,128)S(1)} collective-permute-done((f32[16,128]{1,0:T(8,128)S(1)}, f32[16,128]{1,0:T(8,128)S(1)}, u32[]{:S(2)}, u32[]{:S(2)}) %collective-permute-start.7) | collective-permute-done | bytes 8224 | tf_op jit(solution)/shard_map/ppermute | solution.py:149
  18.9 3.8 %collective-permute-done.3 = f32[16,128]{1,0:T(8,128)S(1)} collective-permute-done((f32[16,128]{1,0:T(8,128)S(1)}, f32[16,128]{1,0:T(8,128)S(1)}, u32[]{:S(2)}, u32[]{:S(2)}) %collective-permute-start.3) | collective-permute-done | bytes 8224 | tf_op jit(solution)/shard_map/ppermute | solution.py:149
  22.7 0.6 %add_add_fusion = f32[16,128]{1,0:T(8,128)} fusion(f32[16,128]{1,0:T(8,128)S(1)} %collective-permute-done.7, f32[16,128]{1,0:T(8,128)S(1)} %collective-permute-done.5, f32[16,128]{1,0:T(8,128)S(1)} %shard_map.48, f32[16,128]{1,0:T(8,128)S(1)} %collective-permute-done.3), kind=kLoop, calls=%fused_computation | loop fusion | flops 6144 | bytes 40960 | tf_op jit(solution)/shard_map/add | solution.py:185
  (3 shorter events, 0.0 us)
Async XLA Ops:
  0.0 11.3 %collective-permute-start = (bf16[128,1024]{1,0:T(8,128)(2,1)}, bf16[128,1024]{1,0:T(8,128)(2,1)S(1)}, u32[]{:S(2)}, u32[]{:S(2)}) collective-permute-start(bf16[128,1024]{1,0:T(8,128)(2,1)} %query_hbm.1), channel_id=1, source_target_pairs={{0,4},{4,0},{8,12},{12,8},{16,20},{20,16},{24,28},{28,24},{1,5},{5... | collective-permute-start | bytes 786440 | tf_op jit(solution)/shard_map/ppermute | solution.py:149
  3.0 8.3 %collective-permute-start.2 = (bf16[128,256]{1,0:T(8,128)(2,1)}, bf16[128,256]{1,0:T(8,128)(2,1)S(1)}, u32[]{:S(2)}, u32[]{:S(2)}) collective-permute-start(bf16[128,256]{1,0:T(8,128)(2,1)} %key_hbm.1), channel_id=1, source_target_pairs={{0,24},{4,28},{8,16},{12,20},{16,8},{20,12},{24,0},{28,4},{1,25},{... | collective-permute-start | bytes 196616 | tf_op jit(solution)/shard_map/ppermute | solution.py:149
  6.6 5.6 %collective-permute-start.4 = (bf16[128,256]{1,0:T(8,128)(2,1)}, bf16[128,256]{1,0:T(8,128)(2,1)S(1)}, u32[]{:S(2)}, u32[]{:S(2)}) collective-permute-start(bf16[128,256]{1,0:T(8,128)(2,1)} %key_hbm.1), channel_id=1, source_target_pairs={{0,16},{4,20},{8,24},{12,28},{16,0},{20,4},{24,8},{28,12},{1,17},{... | collective-permute-start | bytes 196616 | tf_op jit(solution)/shard_map/ppermute | solution.py:149
  6.6 8.0 %collective-permute-start.6 = (bf16[128,256]{1,0:T(8,128)(2,1)}, bf16[128,256]{1,0:T(8,128)(2,1)S(1)}, u32[]{:S(2)}, u32[]{:S(2)}) collective-permute-start(bf16[128,256]{1,0:T(8,128)(2,1)} %key_hbm.1), channel_id=1, source_target_pairs={{0,8},{4,12},{8,0},{12,4},{16,24},{20,28},{24,16},{28,20},{1,9},{5... | collective-permute-start | bytes 196616 | tf_op jit(solution)/shard_map/ppermute | solution.py:149
  7.4 3.9 %collective-permute-start.1 = (f32[16,128]{1,0:T(8,128)}, f32[16,128]{1,0:T(8,128)S(1)}, u32[]{:S(2)}, u32[]{:S(2)}) collective-permute-start(f32[16,128]{1,0:T(8,128)} %lse_hbm.1), channel_id=1, source_target_pairs={{0,4},{4,0},{8,12},{12,8},{16,20},{20,16},{24,28},{28,24},{1,5},{5... | collective-permute-start | bytes 24584 | tf_op jit(solution)/shard_map/ppermute | solution.py:149
  12.2 5.6 %collective-permute-start.5 = (f32[16,128]{1,0:T(8,128)S(1)}, f32[16,128]{1,0:T(8,128)S(1)}, u32[]{:S(2)}, u32[]{:S(2)}) collective-permute-start(f32[16,128]{1,0:T(8,128)S(1)} %shard_map.49), channel_id=1, source_target_pairs={{0,16},{4,20},{8,24},{12,28},{16,0},{20,4},{24,8},{28,12},{1,17},{... | collective-permute-start | bytes 24584 | tf_op jit(solution)/shard_map/ppermute | solution.py:149
  14.6 4.3 %collective-permute-start.7 = (f32[16,128]{1,0:T(8,128)S(1)}, f32[16,128]{1,0:T(8,128)S(1)}, u32[]{:S(2)}, u32[]{:S(2)}) collective-permute-start(f32[16,128]{1,0:T(8,128)S(1)} %shard_map.51), channel_id=1, source_target_pairs={{0,8},{4,12},{8,0},{12,4},{16,24},{20,28},{24,16},{28,20},{1,9},{5... | collective-permute-start | bytes 24584 | tf_op jit(solution)/shard_map/ppermute | solution.py:149
  17.3 5.4 %collective-permute-start.3 = (f32[16,128]{1,0:T(8,128)S(1)}, f32[16,128]{1,0:T(8,128)S(1)}, u32[]{:S(2)}, u32[]{:S(2)}) collective-permute-start(f32[16,128]{1,0:T(8,128)S(1)} %get-tuple-element.16), channel_id=1, source_target_pairs={{0,16},{4,20},{8,24},{12,28},{16,8},{20,12},{24,0},{28,4},{1,17},{... | collective-permute-start | bytes 24584 | tf_op jit(solution)/shard_map/ppermute | solution.py:149
